TPU v7x, 32 devices: a whole 2x2x4 slice. The times are simulated.
32 devices in a mesh: cond: 2 (over x), gx: 4 (over y, core), yz: 4 (over z).
Axes of the slice: x: 2, y: 2, z: 4, core: 2. Of those that a mesh axis runs over, the one named last changes fastest.
Arguments:
- adjoint: float32 [2, 5, 32, 64, 256], P('cond', None, 'gx', 'yz'), may hold values from -6 to 6
- objective_gradient: float32 [2, 5, 32, 64, 256], P('cond', None, 'gx', 'yz'), may hold values from -6 to 6
- diagonal: float32 [32, 64, 256], P('gx', 'yz'), may hold values from 4 to 12
- flux_blocks: float32 [2, 6, 5, 5], P('cond'), may hold values from -1 to 1
- flux_sensitivity: bfloat16 [2, 5, 32, 64, 256], P('cond', None, 'gx', 'yz'), may hold values from -6 to 6
- surface_mask: int32 [32, 64, 256], P('gx', 'yz'), may hold values 0 or 1
- patch_band_slot: int32 [32, 64], P('gx', 'yz'), may hold values from 0 to 62
- design_basis: float32 [256, 128], replicated, may hold values from -0.046875 to 0.046875
- condition_weights: int32 [2], replicated, may hold values from 1 to 999, as said below
Outputs:
- smoothed: float32 [2, 5, 32, 64, 256], P('cond', None, 'gx', 'yz')
- residual: float32 [2, 5, 32, 64, 256], P('cond', None, 'gx', 'yz')
- design_gradient: float32 [4096], P(('gx', 'yz'))
Inputs may be any that keep to these rules, and one draw needn't show every extreme that they name: `condition_weights`: positive integer weights; one condition has weight 999.
All inputs are finite; a program needn't handle non-finite values. No bound on the sum of `surface_mask` on one device may be relied on, other than what follows from the above.
Results may differ from a plain program's by a relative error of at most 0.0003.
Values sent between devices are 32-bit elements; how exact they have to be, the bound alone decides.
A program may use at most 64 MiB of HBM per device.

v0:
```python
import jax
import jax.numpy as jnp
from jax import lax
from jax.sharding import PartitionSpec as P

NDES = 4096
relaxation = 0.8
neighbour_starts = ((2, 1, 1), (0, 1, 1), (1, 2, 1), (1, 0, 1), (1, 1, 2), (1, 1, 0))


def with_halo(block, sides, width):
    for axis, dim in sides:
        count = lax.axis_size(axis)
        forward = [(i, i + 1) for i in range(count - 1)]
        backward = [(target, source) for source, target in forward]
        low = lax.ppermute(
            lax.slice_in_dim(block, block.shape[dim] - width, None, axis=dim), axis, forward
        )
        high = lax.ppermute(lax.slice_in_dim(block, 0, width, axis=dim), axis, backward)
        block = jnp.concatenate([low, block, high], axis=dim)
    return block


def apply_operator(padded_field, diagonal, blocks):
    size_x = padded_field.shape[1] - 2
    size_y = padded_field.shape[2] - 2
    size_z = padded_field.shape[3] - 2
    result = diagonal * padded_field[:, 1:-1, 1:-1, 1:-1]
    for direction in range(6):
        start_x, start_y, start_z = neighbour_starts[direction]
        shifted = padded_field[
            :, start_x : start_x + size_x, start_y : start_y + size_y, start_z : start_z + size_z
        ]
        result = result - jnp.einsum(
            "ec,exyz->cxyz", blocks[direction], shifted, precision=lax.Precision.HIGHEST
        )
    return result


def spread_bands(slot_lookup):
    halfway = slot_lookup.shape[1] // 2
    first_half = jnp.pad(slot_lookup[:, :halfway], ((0, 1), (0, 0)))
    second_half = jnp.pad(slot_lookup[:, halfway:], ((1, 0), (0, 0)))
    return (first_half + second_half).reshape(-1)


def pad_third(values):
    return jnp.pad(values, ((0, 0), (0, 0), (0, 0), (1, 1)))


def local(
    adjoint,
    objective_gradient,
    diagonal,
    flux_blocks,
    flux_sensitivity,
    surface_mask,
    patch_band_slot,
    design_basis,
    condition_weights,
):
    blocks = flux_blocks[0]
    source = objective_gradient[0]
    start_field = adjoint[0]

    def operate(values):
        haloed = with_halo(values, (("gx", 1), ("yz", 2)), 1)
        return apply_operator(pad_third(haloed), diagonal, blocks)

    relaxed = start_field + relaxation * (source - operate(start_field)) / diagonal
    smoothed = relaxed + relaxation * (source - operate(relaxed)) / diagonal
    residual = source - operate(smoothed)
    surface = surface_mask.astype(jnp.float32) * jnp.sum(
        smoothed * flux_sensitivity[0].astype(jnp.float32), axis=0
    )
    projected_gradient = jnp.dot(
        surface.reshape(-1, surface.shape[-1]),
        design_basis,
        precision=lax.Precision.HIGHEST,
        preferred_element_type=jnp.float32,
    )
    slot_count = 2 * NDES // design_basis.shape[1] - 1
    onehot = (jnp.arange(slot_count)[:, None] == patch_band_slot.reshape(1, -1)).astype(jnp.float32)
    slot_lookup = jnp.dot(
        onehot,
        projected_gradient,
        precision=lax.Precision.HIGHEST,
        preferred_element_type=jnp.float32,
    )
    gradient = spread_bands(slot_lookup)
    weights_float = condition_weights.astype(jnp.float32)
    picked = jnp.arange(weights_float.shape[0]) == lax.axis_index("cond")
    local_portion = jnp.sum(jnp.where(picked, weights_float, 0.0)) / jnp.sum(weights_float)
    summed = lax.psum(local_portion * gradient, ("cond", "gx", "yz"))
    pieces = NDES // lax.axis_size(("gx", "yz"))
    design_gradient = lax.dynamic_slice_in_dim(
        summed, lax.axis_index(("gx", "yz")) * pieces, pieces, 0
    )
    return (smoothed[None], residual[None], design_gradient)


def solution(mesh):
    placed = (
        P("cond", None, "gx", "yz", None),
        P("cond", None, "gx", "yz", None),
        P("gx", "yz", None),
        P("cond", None, None, None),
        P("cond", None, "gx", "yz", None),
        P("gx", "yz", None),
        P("gx", "yz"),
        P(),
        P(),
    )
    return jax.shard_map(
        local,
        mesh=mesh,
        in_specs=placed,
        out_specs=(
            P("cond", None, "gx", "yz", None),
            P("cond", None, "gx", "yz", None),
            P(("gx", "yz")),
        ),
        check_vma=False,
    )
```

profile of v0, /device:TPU:12, one launch (start us, length us, event | category | flops | bytes accessed | tf_op | source)
XLA Modules:
  0.0 115.4 jit_solution(11190379338171602337)
XLA Ops:
  0.7 1.5 %copy.88 = f32[1,5,8,16,256]{4,1,3,2,0:T(8,128)S(1)} copy(f32[1,5,8,16,256]{4,3,2,1,0:T(8,128)} %param.9) | data formatting | bytes 1310720 | tf_op args[0]
  2.2 1.9 %collective-permute-start = (f32[5,1,16,256]{3,0,2,1:T(8,128)S(1)}, f32[5,1,16,256]{3,0,2,1:T(8,128)S(1)}, u32[]{:S(2)}, u32[]{:S(2)}) collective-permute-start(f32[5,1,16,256]{3,0,2,1:T(8,128)S(1)} %get-tuple-element.19), channel_id=1, source_target_pairs={{4,0},{8,4},{12,8},{5,1},{9,5},{13,9},{6,2},{10,6},{14,10},{7,3},{... | collective-permute-start | bytes 245768 | tf_op jit(solution)/shard_map/ppermute | solution.py:19
  4.1 2.4 %collective-permute-start.1 = (f32[5,1,16,256]{3,0,2,1:T(8,128)S(1)}, f32[5,1,16,256]{3,0,2,1:T(8,128)S(1)}, u32[]{:S(2)}, u32[]{:S(2)}) collective-permute-start(f32[5,1,16,256]{3,0,2,1:T(8,128)S(1)} %get-tuple-element.18), channel_id=1, source_target_pairs={{0,4},{4,8},{8,12},{1,5},{5,9},{9,13},{2,6},{6,10},{10,14},{3,7},{... | collective-permute-start | bytes 245768 | tf_op jit(solution)/shard_map/ppermute | solution.py:16
  7.7 2.8 %collective-permute-done.1 = f32[5,1,16,256]{3,0,2,1:T(8,128)S(1)} collective-permute-done((f32[5,1,16,256]{3,0,2,1:T(8,128)S(1)}, f32[5,1,16,256]{3,0,2,1:T(8,128)S(1)}, u32[]{:S(2)}, u32[]{:S(2)}) %collective-permute-start.1) | collective-permute-done | bytes 81952 | tf_op jit(solution)/shard_map/ppermute | solution.py:16
  10.4 2.4 %collective-permute-start.2 = (f32[5,10,1,256]{3,0,2,1:T(8,128)S(1)}, f32[5,10,1,256]{3,0,2,1:T(8,128)S(1)}, u32[]{:S(2)}, u32[]{:S(2)}) collective-permute-start(f32[5,10,1,256]{3,0,2,1:T(8,128)S(1)} %get-tuple-element.13), channel_id=1, source_target_pairs={{1,0},{2,1},{3,2},{5,4},{6,5},{7,6},{9,8},{10,9},{11,10},{13,12},{... | collective-permute-start | bytes 153608 | tf_op jit(solution)/shard_map/ppermute | solution.py:19
  12.8 3.5 %collective-permute-start.3 = (f32[5,10,1,256]{3,0,2,1:T(8,128)S(1)}, f32[5,10,1,256]{3,0,2,1:T(8,128)S(1)}, u32[]{:S(2)}, u32[]{:S(2)}) collective-permute-start(f32[5,10,1,256]{3,0,2,1:T(8,128)S(1)} %get-tuple-element.12), channel_id=1, source_target_pairs={{0,1},{1,2},{2,3},{4,5},{5,6},{6,7},{8,9},{9,10},{10,11},{12,13},{... | collective-permute-start | bytes 153608 | tf_op jit(solution)/shard_map/ppermute | solution.py:16
  16.3 1.1 convolution_bitcast_fusion.4
  17.4 1.8 %collective-permute-done.3 = f32[5,10,1,256]{3,0,2,1:T(8,128)S(1)} collective-permute-done((f32[5,10,1,256]{3,0,2,1:T(8,128)S(1)}, f32[5,10,1,256]{3,0,2,1:T(8,128)S(1)}, u32[]{:S(2)}, u32[]{:S(2)}) %collective-permute-start.3) | collective-permute-done | bytes 51232 | tf_op jit(solution)/shard_map/ppermute | solution.py:16
  20.9 1.2 %convolution_bitcast_fusion.11 = f32[5,8,16,256]{3,0,2,1:T(8,128)S(1)} fusion(f32[5,10,18,258]{3,0,2,1:T(8,128)S(1)} %select_maximum_fusion.8, f32[1,1,5,5]{3,2,1,0:T(8,128)S(1)} %copy.81), kind=kOutput, calls=%fused_computation.86 | convolution fusion | flops 9830400 | bytes 1708032 | tf_op jit(solution)/shard_map/ec,exyz->cxyz/dot_general | solution.py:34
  22.1 1.1 fusion.61
  23.2 1.1 fusion.64
  24.3 2.0 %fusion.94 = f32[5,8,16,256]{3,0,2,1:T(8,128)S(1)} fusion(f32[5,8,16,256]{3,0,2,1:T(8,128)S(1)} %bitcast.184, f32[5,8,16,256]{3,0,2,1:T(8,128)S(1)} %convolution_bitcast_fusion.10, f32[5,8,16,256]{3,0,2,1:T(8,128)S(1)} %convolution_bitcast_fusion.11, f32[5,8,16,256]{3,0,2,1:T(8,128)S(1)} %fusion.61, f32[5,8,16,256]{3,0,2,1:T(8,128)S(1)} %fusion.64, ...), kind=kOutput, calls=%fused_computation.108 | convolution fusion | flops 11816960 | bytes 5455972 | tf_op jit(solution)/shard_map/ec,exyz->cxyz/dot_general | solution.py:34
  26.3 1.9 %collective-permute-start.4 = (f32[5,1,16,256]{3,0,2,1:T(8,128)S(1)}, f32[5,1,16,256]{3,0,2,1:T(8,128)S(1)}, u32[]{:S(2)}, u32[]{:S(2)}) collective-permute-start(f32[5,1,16,256]{3,0,2,1:T(8,128)S(1)} %get-tuple-element.17), channel_id=1, source_target_pairs={{4,0},{8,4},{12,8},{5,1},{9,5},{13,9},{6,2},{10,6},{14,10},{7,3},{... | collective-permute-start | bytes 245768 | tf_op jit(solution)/shard_map/ppermute | solution.py:19
  28.3 2.4 %collective-permute-start.5 = (f32[5,1,16,256]{3,0,2,1:T(8,128)S(1)}, f32[5,1,16,256]{3,0,2,1:T(8,128)S(1)}, u32[]{:S(2)}, u32[]{:S(2)}) collective-permute-start(f32[5,1,16,256]{3,0,2,1:T(8,128)S(1)} %get-tuple-element.16), channel_id=1, source_target_pairs={{0,4},{4,8},{8,12},{1,5},{5,9},{9,13},{2,6},{6,10},{10,14},{3,7},{... | collective-permute-start | bytes 245768 | tf_op jit(solution)/shard_map/ppermute | solution.py:16
  32.7 1.9 %collective-permute-done.5 = f32[5,1,16,256]{3,0,2,1:T(8,128)S(1)} collective-permute-done((f32[5,1,16,256]{3,0,2,1:T(8,128)S(1)}, f32[5,1,16,256]{3,0,2,1:T(8,128)S(1)}, u32[]{:S(2)}, u32[]{:S(2)}) %collective-permute-start.5) | collective-permute-done | bytes 81952 | tf_op jit(solution)/shard_map/ppermute | solution.py:16
  34.6 1.9 %collective-permute-start.6 = (f32[5,10,1,256]{3,0,2,1:T(8,128)S(1)}, f32[5,10,1,256]{3,0,2,1:T(8,128)S(1)}, u32[]{:S(2)}, u32[]{:S(2)}) collective-permute-start(f32[5,10,1,256]{3,0,2,1:T(8,128)S(1)} %get-tuple-element.11), channel_id=1, source_target_pairs={{1,0},{2,1},{3,2},{5,4},{6,5},{7,6},{9,8},{10,9},{11,10},{13,12},{... | collective-permute-start | bytes 153608 | tf_op jit(solution)/shard_map/ppermute | solution.py:19
  36.5 4.1 %collective-permute-start.7 = (f32[5,10,1,256]{3,0,2,1:T(8,128)S(1)}, f32[5,10,1,256]{3,0,2,1:T(8,128)S(1)}, u32[]{:S(2)}, u32[]{:S(2)}) collective-permute-start(f32[5,10,1,256]{3,0,2,1:T(8,128)S(1)} %get-tuple-element.10), channel_id=1, source_target_pairs={{0,1},{1,2},{2,3},{4,5},{5,6},{6,7},{8,9},{9,10},{10,11},{12,13},{... | collective-permute-start | bytes 153608 | tf_op jit(solution)/shard_map/ppermute | solution.py:16
  41.7 1.1 collective-permute-done.7
  44.5 1.2 %convolution_bitcast_fusion.9 = f32[5,8,16,256]{3,0,2,1:T(8,128)S(1)} fusion(f32[5,10,18,258]{3,0,2,1:T(8,128)S(1)} %select_maximum_fusion.4, f32[1,1,5,5]{3,2,1,0:T(8,128)S(1)} %copy.81), kind=kOutput, calls=%fused_computation.84 | convolution fusion | flops 9830400 | bytes 1708032 | tf_op jit(solution)/shard_map/ec,exyz->cxyz/dot_general | solution.py:34
  45.8 1.1 fusion.55
  46.9 1.1 fusion.58
  47.9 2.2 %fusion.119 = (f32[8,16,256]{2,1,0:T(8,128)S(1)}, f32[5,8,16,256]{3,0,2,1:T(8,128)S(1)}) fusion(bf16[1,5,8,16,256]{4,3,2,1,0:T(8,128)(2,1)S(1)} %copy-done.3, f32[5,8,16,256]{3,0,2,1:T(8,128)S(1)} %fusion.94, f32[5,8,16,256]{3,0,2,1:T(8,128)S(1)} %convolution_bitcast_fusion.8, f32[5,8,16,256]{3,0,2,1:T(8,128)S(1)} %convolution_bitcast_fusion.9, ...), kind=kOutput, calls=%fused_computation.134 | convolution fusion | flops 12275712 | bytes 5914724 | tf_op jit(solution)/shard_map/ec,exyz->cxyz/dot_general | solution.py:34
  51.2 1.9 %collective-permute-start.8 = (f32[5,1,16,256]{3,0,2,1:T(8,128)S(1)}, f32[5,1,16,256]{3,0,2,1:T(8,128)S(1)}, u32[]{:S(2)}, u32[]{:S(2)}) collective-permute-start(f32[5,1,16,256]{3,0,2,1:T(8,128)S(1)} %get-tuple-element.15), channel_id=1, source_target_pairs={{4,0},{8,4},{12,8},{5,1},{9,5},{13,9},{6,2},{10,6},{14,10},{7,3},{... | collective-permute-start | bytes 245768 | tf_op jit(solution)/shard_map/ppermute | solution.py:19
  53.1 2.4 %collective-permute-start.9 = (f32[5,1,16,256]{3,0,2,1:T(8,128)S(1)}, f32[5,1,16,256]{3,0,2,1:T(8,128)S(1)}, u32[]{:S(2)}, u32[]{:S(2)}) collective-permute-start(f32[5,1,16,256]{3,0,2,1:T(8,128)S(1)} %get-tuple-element.14), channel_id=1, source_target_pairs={{0,4},{4,8},{8,12},{1,5},{5,9},{9,13},{2,6},{6,10},{10,14},{3,7},{... | collective-permute-start | bytes 245768 | tf_op jit(solution)/shard_map/ppermute | solution.py:16
  56.2 41.7 %psum.7 = f32[4096]{0:T(1024)S(1)} all-reduce(f32[4096]{0:T(1024)S(1)} %mul.57), channel_id=1, replica_groups=mesh['cond'=2,'gx'=4,'yz'=4] {'cond','gx','yz'}, use_global_device_ids=true, to_apply=%region_3.4 | all-reduce | flops 4096 | bytes 32768 | tf_op jit(solution)/shard_map/psum | solution.py:94
  98.5 2.4 %collective-permute-start.10 = (f32[5,10,1,256]{3,0,2,1:T(8,128)S(1)}, f32[5,10,1,256]{3,0,2,1:T(8,128)S(1)}, u32[]{:S(2)}, u32[]{:S(2)}) collective-permute-start(f32[5,10,1,256]{3,0,2,1:T(8,128)S(1)} %get-tuple-element.9), channel_id=1, source_target_pairs={{1,0},{2,1},{3,2},{5,4},{6,5},{7,6},{9,8},{10,9},{11,10},{13,12},{... | collective-permute-start | bytes 153608 | tf_op jit(solution)/shard_map/ppermute | solution.py:19
  101.0 3.6 %collective-permute-start.11 = (f32[5,10,1,256]{3,0,2,1:T(8,128)S(1)}, f32[5,10,1,256]{3,0,2,1:T(8,128)S(1)}, u32[]{:S(2)}, u32[]{:S(2)}) collective-permute-start(f32[5,10,1,256]{3,0,2,1:T(8,128)S(1)} %get-tuple-element.8), channel_id=1, source_target_pairs={{0,1},{1,2},{2,3},{4,5},{5,6},{6,7},{8,9},{9,10},{10,11},{12,13},{... | collective-permute-start | bytes 153608 | tf_op jit(solution)/shard_map/ppermute | solution.py:16
  104.6 1.1 convolution_bitcast_fusion
  105.7 1.6 %collective-permute-done.11 = f32[5,10,1,256]{3,0,2,1:T(8,128)S(1)} collective-permute-done((f32[5,10,1,256]{3,0,2,1:T(8,128)S(1)}, f32[5,10,1,256]{3,0,2,1:T(8,128)S(1)}, u32[]{:S(2)}, u32[]{:S(2)}) %collective-permute-start.11) | collective-permute-done | bytes 51232 | tf_op jit(solution)/shard_map/ppermute | solution.py:16
  109.0 1.2 %convolution_bitcast_fusion.7 = f32[5,8,16,256]{3,0,2,1:T(8,128)S(1)} fusion(f32[5,10,18,258]{3,0,2,1:T(8,128)S(1)} %select_maximum_fusion, f32[1,1,5,5]{3,2,1,0:T(8,128)S(1)} %copy.81), kind=kOutput, calls=%fused_computation.82 | convolution fusion | flops 9830400 | bytes 1708032 | tf_op jit(solution)/shard_map/ec,exyz->cxyz/dot_general | solution.py:34
  111.3 1.1 fusion.52
  112.4 2.0 %fusion.86 = f32[1,5,8,16,256]{4,1,3,2,0:T(8,128)S(1)} fusion(f32[5,8,16,256]{3,0,2,1:T(8,128)S(1)} %convolution_bitcast_fusion.6, f32[5,8,16,256]{3,0,2,1:T(8,128)S(1)} %convolution_bitcast_fusion.7, f32[5,8,16,256]{3,0,2,1:T(8,128)S(1)} %fusion.49, f32[5,8,16,256]{3,0,2,1:T(8,128)S(1)} %fusion.52, f32[5,8,16,256]{3,0,2,1:T(8,128)S(1)} %convolution_bitcast_fusion, ...), kind=kOutput, calls=%fused_computation.100 | convolution fusion | flops 11325440 | bytes 5455972 | tf_op jit(solution)/shard_map/ec,exyz->cxyz/dot_general | solution.py:34
  (55 shorter events, 12.4 us)
Async XLA Ops:
  0.6 54.9 %copy-start = (f32[256,128]{1,0:T(8,128)S(1)}, f32[256,128]{1,0:T(8,128)}, u32[]{:S(2)}) copy-start(f32[256,128]{1,0:T(8,128)} %param.16) | copy-start | bytes 393220
  0.6 5.9 %copy-start.4 = (f32[1,6,5,5]{1,0,3,2:T(1,128)S(1)}, f32[1,6,5,5]{1,0,3,2:T(1,128)}, u32[]{:S(2)}) copy-start(f32[1,6,5,5]{1,0,3,2:T(1,128)} %param.12) | copy-start | bytes 1804
  0.7 6.9 %copy-start.6 = (s32[8,16]{1,0:T(8,128)S(1)}, s32[8,16]{1,0:T(8,128)}, u32[]{:S(2)}) copy-start(s32[8,16]{1,0:T(8,128)} %param.15) | copy-start | bytes 1540
  2.2 5.4 %collective-permute-start = (f32[5,1,16,256]{3,0,2,1:T(8,128)S(1)}, f32[5,1,16,256]{3,0,2,1:T(8,128)S(1)}, u32[]{:S(2)}, u32[]{:S(2)}) collective-permute-start(f32[5,1,16,256]{3,0,2,1:T(8,128)S(1)} %get-tuple-element.19), channel_id=1, source_target_pairs={{4,0},{8,4},{12,8},{5,1},{9,5},{13,9},{6,2},{10,6},{14,10},{7,3},{... | collective-permute-start | bytes 245768 | tf_op jit(solution)/shard_map/ppermute | solution.py:19
  4.1 6.3 %collective-permute-start.1 = (f32[5,1,16,256]{3,0,2,1:T(8,128)S(1)}, f32[5,1,16,256]{3,0,2,1:T(8,128)S(1)}, u32[]{:S(2)}, u32[]{:S(2)}) collective-permute-start(f32[5,1,16,256]{3,0,2,1:T(8,128)S(1)} %get-tuple-element.18), channel_id=1, source_target_pairs={{0,4},{4,8},{8,12},{1,5},{5,9},{9,13},{2,6},{6,10},{10,14},{3,7},{... | collective-permute-start | bytes 245768 | tf_op jit(solution)/shard_map/ppermute | solution.py:16
  10.4 6.9 %collective-permute-start.2 = (f32[5,10,1,256]{3,0,2,1:T(8,128)S(1)}, f32[5,10,1,256]{3,0,2,1:T(8,128)S(1)}, u32[]{:S(2)}, u32[]{:S(2)}) collective-permute-start(f32[5,10,1,256]{3,0,2,1:T(8,128)S(1)} %get-tuple-element.13), channel_id=1, source_target_pairs={{1,0},{2,1},{3,2},{5,4},{6,5},{7,6},{9,8},{10,9},{11,10},{13,12},{... | collective-permute-start | bytes 153608 | tf_op jit(solution)/shard_map/ppermute | solution.py:19
  12.8 6.3 %collective-permute-start.3 = (f32[5,10,1,256]{3,0,2,1:T(8,128)S(1)}, f32[5,10,1,256]{3,0,2,1:T(8,128)S(1)}, u32[]{:S(2)}, u32[]{:S(2)}) collective-permute-start(f32[5,10,1,256]{3,0,2,1:T(8,128)S(1)} %get-tuple-element.12), channel_id=1, source_target_pairs={{0,1},{1,2},{2,3},{4,5},{5,6},{6,7},{8,9},{9,10},{10,11},{12,13},{... | collective-permute-start | bytes 153608 | tf_op jit(solution)/shard_map/ppermute | solution.py:16
  22.1 2.2 %copy-start.1 = (f32[1,5,8,16,256]{4,3,2,1,0:T(8,128)S(1)}, f32[1,5,8,16,256]{4,3,2,1,0:T(8,128)}, u32[]{:S(2)}) copy-start(f32[1,5,8,16,256]{4,3,2,1,0:T(8,128)} %param.10) | copy-start | bytes 1966084
  22.1 2.2 %copy-start.2 = (f32[8,16,256]{2,1,0:T(8,128)S(1)}, f32[8,16,256]{2,1,0:T(8,128)}, u32[]{:S(2)}) copy-start(f32[8,16,256]{2,1,0:T(8,128)} %param.11) | copy-start | bytes 393220
  24.3 6.4 %copy-start.7 = (s32[2]{0:T(128)S(1)}, s32[2]{0:T(128)}, u32[]{:S(2)}) copy-start(s32[2]{0:T(128)} %param.17) | copy-start | bytes 28
  26.3 6.3 %collective-permute-start.4 = (f32[5,1,16,256]{3,0,2,1:T(8,128)S(1)}, f32[5,1,16,256]{3,0,2,1:T(8,128)S(1)}, u32[]{:S(2)}, u32[]{:S(2)}) collective-permute-start(f32[5,1,16,256]{3,0,2,1:T(8,128)S(1)} %get-tuple-element.17), channel_id=1, source_target_pairs={{4,0},{8,4},{12,8},{5,1},{9,5},{13,9},{6,2},{10,6},{14,10},{7,3},{... | collective-permute-start | bytes 245768 | tf_op jit(solution)/shard_map/ppermute | solution.py:19
  28.3 6.3 %collective-permute-start.5 = (f32[5,1,16,256]{3,0,2,1:T(8,128)S(1)}, f32[5,1,16,256]{3,0,2,1:T(8,128)S(1)}, u32[]{:S(2)}, u32[]{:S(2)}) collective-permute-start(f32[5,1,16,256]{3,0,2,1:T(8,128)S(1)} %get-tuple-element.16), channel_id=1, source_target_pairs={{0,4},{4,8},{8,12},{1,5},{5,9},{9,13},{2,6},{6,10},{10,14},{3,7},{... | collective-permute-start | bytes 245768 | tf_op jit(solution)/shard_map/ppermute | solution.py:16
  34.6 7.1 %collective-permute-start.6 = (f32[5,10,1,256]{3,0,2,1:T(8,128)S(1)}, f32[5,10,1,256]{3,0,2,1:T(8,128)S(1)}, u32[]{:S(2)}, u32[]{:S(2)}) collective-permute-start(f32[5,10,1,256]{3,0,2,1:T(8,128)S(1)} %get-tuple-element.11), channel_id=1, source_target_pairs={{1,0},{2,1},{3,2},{5,4},{6,5},{7,6},{9,8},{10,9},{11,10},{13,12},{... | collective-permute-start | bytes 153608 | tf_op jit(solution)/shard_map/ppermute | solution.py:19
  36.5 6.3 %collective-permute-start.7 = (f32[5,10,1,256]{3,0,2,1:T(8,128)S(1)}, f32[5,10,1,256]{3,0,2,1:T(8,128)S(1)}, u32[]{:S(2)}, u32[]{:S(2)}) collective-permute-start(f32[5,10,1,256]{3,0,2,1:T(8,128)S(1)} %get-tuple-element.10), channel_id=1, source_target_pairs={{0,1},{1,2},{2,3},{4,5},{5,6},{6,7},{8,9},{9,10},{10,11},{12,13},{... | collective-permute-start | bytes 153608 | tf_op jit(solution)/shard_map/ppermute | solution.py:16
  45.8 2.2 %copy-start.3 = (bf16[1,5,8,16,256]{4,3,2,1,0:T(8,128)(2,1)S(1)}, bf16[1,5,8,16,256]{4,3,2,1,0:T(8,128)(2,1)}, u32[]{:S(2)}) copy-start(bf16[1,5,8,16,256]{4,3,2,1,0:T(8,128)(2,1)} %param.13) | copy-start | bytes 983044
  50.1 5.4 %copy-start.5 = (s32[8,16,256]{2,1,0:T(8,128)S(1)}, s32[8,16,256]{2,1,0:T(8,128)}, u32[]{:S(2)}) copy-start(s32[8,16,256]{2,1,0:T(8,128)} %param.14) | copy-start | bytes 393220
  51.2 47.3 %collective-permute-start.8 = (f32[5,1,16,256]{3,0,2,1:T(8,128)S(1)}, f32[5,1,16,256]{3,0,2,1:T(8,128)S(1)}, u32[]{:S(2)}, u32[]{:S(2)}) collective-permute-start(f32[5,1,16,256]{3,0,2,1:T(8,128)S(1)} %get-tuple-element.15), channel_id=1, source_target_pairs={{4,0},{8,4},{12,8},{5,1},{9,5},{13,9},{6,2},{10,6},{14,10},{7,3},{... | collective-permute-start | bytes 245768 | tf_op jit(solution)/shard_map/ppermute | solution.py:19
  53.1 45.4 %collective-permute-start.9 = (f32[5,1,16,256]{3,0,2,1:T(8,128)S(1)}, f32[5,1,16,256]{3,0,2,1:T(8,128)S(1)}, u32[]{:S(2)}, u32[]{:S(2)}) collective-permute-start(f32[5,1,16,256]{3,0,2,1:T(8,128)S(1)} %get-tuple-element.14), channel_id=1, source_target_pairs={{0,4},{4,8},{8,12},{1,5},{5,9},{9,13},{2,6},{6,10},{10,14},{3,7},{... | collective-permute-start | bytes 245768 | tf_op jit(solution)/shard_map/ppermute | solution.py:16
  98.5 7.2 %collective-permute-start.10 = (f32[5,10,1,256]{3,0,2,1:T(8,128)S(1)}, f32[5,10,1,256]{3,0,2,1:T(8,128)S(1)}, u32[]{:S(2)}, u32[]{:S(2)}) collective-permute-start(f32[5,10,1,256]{3,0,2,1:T(8,128)S(1)} %get-tuple-element.9), channel_id=1, source_target_pairs={{1,0},{2,1},{3,2},{5,4},{6,5},{7,6},{9,8},{10,9},{11,10},{13,12},{... | collective-permute-start | bytes 153608 | tf_op jit(solution)/shard_map/ppermute | solution.py:19
  101.0 6.3 %collective-permute-start.11 = (f32[5,10,1,256]{3,0,2,1:T(8,128)S(1)}, f32[5,10,1,256]{3,0,2,1:T(8,128)S(1)}, u32[]{:S(2)}, u32[]{:S(2)}) collective-permute-start(f32[5,10,1,256]{3,0,2,1:T(8,128)S(1)} %get-tuple-element.8), channel_id=1, source_target_pairs={{0,1},{1,2},{2,3},{4,5},{5,6},{6,7},{8,9},{9,10},{10,11},{12,13},{... | collective-permute-start | bytes 153608 | tf_op jit(solution)/shard_map/ppermute | solution.py:16
where the time goes:
time: 116 us; the launch traced here: 115 us
  blocking collectives  41.7 us (36%)
  starting transfers between devices  30.9 us (27%)
  matrix products  23 us (20%)
  waiting for transfers between devices  9.19 us (8%)
  local copies, waits for them, and re-layouts  5.56 us (5%)
  other arithmetic  2.64 us (2%)
  between operations  2.47 us (2%)
    psum x1, blocking collectives, local(): summed = lax.psum(local_portion * gradient, ('cond', 'gx', 'yz'))  41.7 us
    dot_general x18, matrix products, apply_operator(): jnp.einsum('ec,exyz->cxyz', blocks[direction], shifted, precision=lax.Pre...  22.6 us
    ppermute x6, starting transfers between devices, with_halo(): lax.ppermute(lax.slice_in_dim(block, block.shape[dim] - width, None, axis...  18.4 us
    ppermute x6, starting transfers between devices, with_halo(): lax.ppermute(lax.slice_in_dim(block, 0, width, axis=dim), axis, backward)  12.5 us
    ppermute x6, waiting for transfers between devices, with_halo(): lax.ppermute(lax.slice_in_dim(block, block.shape[dim] - width, None, axis...  9.18 us
    unnamed x25, local copies, waits for them, and re-layouts  4.43 us
  transfers between devices with their start and end apart: 12, of which 5 were waited for; matrix products, arithmetic and copies ran while one was open for 5% of the time, Pallas kernels for 0%

commit v1 on v0

--- a/solution.py
+++ b/solution.py
@@ -91,7 +91,7 @@
     weights_float = condition_weights.astype(jnp.float32)
     picked = jnp.arange(weights_float.shape[0]) == lax.axis_index("cond")
     local_portion = jnp.sum(jnp.where(picked, weights_float, 0.0)) / jnp.sum(weights_float)
-    summed = lax.psum(local_portion * gradient, ("cond", "gx", "yz"))
+    summed = jnp.sum(lax.all_gather(local_portion * gradient, ("cond", "gx", "yz")), axis=0)
     pieces = NDES // lax.axis_size(("gx", "yz"))
     design_gradient = lax.dynamic_slice_in_dim(
         summed, lax.axis_index(("gx", "yz")) * pieces, pieces, 0

time: 116 us -> 148 us (1.28)
  the two profiles are of different devices: /device:TPU:12 before, /device:TPU:0 now
where the time goes in v1:
time: 148 us
  blocking collectives  75.7 us (51%)
  starting transfers between devices  35.3 us (24%)
  matrix products  23 us (16%)
  local copies, waits for them, and re-layouts  5.57 us (4%)
  other arithmetic  2.99 us (2%)
  between operations  2.49 us (2%)
  waiting for transfers between devices  2.47 us (2%)
    all_gather x1, blocking collectives, local(): lax.all_gather(local_portion * gradient, ('cond', 'gx', 'yz'))  75.7 us
    ppermute x6, starting transfers between devices, with_halo(): lax.ppermute(lax.slice_in_dim(block, block.shape[dim] - width, None, axis...  27.6 us
    dot_general x18, matrix products, apply_operator(): jnp.einsum('ec,exyz->cxyz', blocks[direction], shifted, precision=lax.Pre...  22.6 us
    ppermute x6, starting transfers between devices, with_halo(): lax.ppermute(lax.slice_in_dim(block, 0, width, axis=dim), axis, backward)  7.75 us
    unnamed x26, local copies, waits for them, and re-layouts  4.51 us
  transfers between devices with their start and end apart: 12, of which 3 were waited for; matrix products, arithmetic and copies ran while one was open for 5% of the time, Pallas kernels for 0%

profile of v1, /device:TPU:0, one launch (start us, length us, event | category | flops | bytes accessed | tf_op | source)
XLA Modules:
  0.0 147.6 jit_solution(14625260624071816642)
XLA Ops:
  0.7 1.5 %copy.117 = f32[1,5,8,16,256]{4,1,3,2,0:T(8,128)S(1)} copy(f32[1,5,8,16,256]{4,3,2,1,0:T(8,128)} %param.9) | data formatting | bytes 1310720 | tf_op args[0]
  2.2 1.3 collective-permute-start
  3.5 3.0 %collective-permute-start.1 = (f32[5,1,16,256]{3,0,2,1:T(8,128)S(1)}, f32[5,1,16,256]{3,0,2,1:T(8,128)S(1)}, u32[]{:S(2)}, u32[]{:S(2)}) collective-permute-start(f32[5,1,16,256]{3,0,2,1:T(8,128)S(1)} %get-tuple-element.21), channel_id=1, source_target_pairs={{0,4},{4,8},{8,12},{1,5},{5,9},{9,13},{2,6},{6,10},{10,14},{3,7},{... | collective-permute-start | bytes 245768 | tf_op jit(solution)/shard_map/ppermute | solution.py:16
  7.7 1.3 collective-permute-start.2
  9.0 5.6 %collective-permute-start.3 = (f32[5,10,1,256]{3,0,2,1:T(8,128)S(1)}, f32[5,10,1,256]{3,0,2,1:T(8,128)S(1)}, u32[]{:S(2)}, u32[]{:S(2)}) collective-permute-start(f32[5,10,1,256]{3,0,2,1:T(8,128)S(1)} %get-tuple-element.15), channel_id=1, source_target_pairs={{0,1},{1,2},{2,3},{4,5},{5,6},{6,7},{8,9},{9,10},{10,11},{12,13},{... | collective-permute-start | bytes 153608 | tf_op jit(solution)/shard_map/ppermute | solution.py:16
  14.6 1.1 convolution_bitcast_fusion.4
  17.3 1.0 convolution_bitcast_fusion.10
  18.3 1.2 convolution_bitcast_fusion.11
  19.6 1.1 fusion.61
  20.7 1.1 fusion.64
  21.8 2.0 %fusion.94 = f32[5,8,16,256]{3,0,2,1:T(8,128)S(1)} fusion(f32[5,8,16,256]{3,0,2,1:T(8,128)S(1)} %bitcast.184, f32[5,8,16,256]{3,0,2,1:T(8,128)S(1)} %convolution_bitcast_fusion.10, f32[5,8,16,256]{3,0,2,1:T(8,128)S(1)} %convolution_bitcast_fusion.11, f32[5,8,16,256]{3,0,2,1:T(8,128)S(1)} %fusion.61, f32[5,8,16,256]{3,0,2,1:T(8,128)S(1)} %fusion.64, ...), kind=kOutput, calls=%fused_computation.108 | convolution fusion | flops 11816960 | bytes 5455972 | tf_op jit(solution)/shard_map/ec,exyz->cxyz/dot_general | solution.py:34
  23.8 1.3 collective-permute-start.4
  25.1 3.8 %collective-permute-start.5 = (f32[5,1,16,256]{3,0,2,1:T(8,128)S(1)}, f32[5,1,16,256]{3,0,2,1:T(8,128)S(1)}, u32[]{:S(2)}, u32[]{:S(2)}) collective-permute-start(f32[5,1,16,256]{3,0,2,1:T(8,128)S(1)} %get-tuple-element.19), channel_id=1, source_target_pairs={{0,4},{4,8},{8,12},{1,5},{5,9},{9,13},{2,6},{6,10},{10,14},{3,7},{... | collective-permute-start | bytes 245768 | tf_op jit(solution)/shard_map/ppermute | solution.py:16
  30.9 1.3 collective-permute-start.6
  32.2 4.8 %collective-permute-start.7 = (f32[5,10,1,256]{3,0,2,1:T(8,128)S(1)}, f32[5,10,1,256]{3,0,2,1:T(8,128)S(1)}, u32[]{:S(2)}, u32[]{:S(2)}) collective-permute-start(f32[5,10,1,256]{3,0,2,1:T(8,128)S(1)} %get-tuple-element.13), channel_id=1, source_target_pairs={{0,1},{1,2},{2,3},{4,5},{5,6},{6,7},{8,9},{9,10},{10,11},{12,13},{... | collective-permute-start | bytes 153608 | tf_op jit(solution)/shard_map/ppermute | solution.py:16
  37.0 1.1 convolution_bitcast_fusion.2
  40.6 1.2 convolution_bitcast_fusion.9
  41.8 1.1 fusion.55
  42.9 1.1 fusion.58
  44.0 2.2 %fusion.119 = (f32[8,16,256]{2,1,0:T(8,128)S(1)}, f32[5,8,16,256]{3,0,2,1:T(8,128)S(1)}) fusion(bf16[1,5,8,16,256]{4,3,2,1,0:T(8,128)(2,1)S(1)} %copy-done.3, f32[5,8,16,256]{3,0,2,1:T(8,128)S(1)} %fusion.94, f32[5,8,16,256]{3,0,2,1:T(8,128)S(1)} %convolution_bitcast_fusion.8, f32[5,8,16,256]{3,0,2,1:T(8,128)S(1)} %convolution_bitcast_fusion.9, ...), kind=kOutput, calls=%fused_computation.134 | convolution fusion | flops 12275712 | bytes 5914724 | tf_op jit(solution)/shard_map/ec,exyz->cxyz/dot_general | solution.py:34
  46.2 1.3 collective-permute-start.8
  47.5 5.6 %collective-permute-start.9 = (f32[5,1,16,256]{3,0,2,1:T(8,128)S(1)}, f32[5,1,16,256]{3,0,2,1:T(8,128)S(1)}, u32[]{:S(2)}, u32[]{:S(2)}) collective-permute-start(f32[5,1,16,256]{3,0,2,1:T(8,128)S(1)} %get-tuple-element.17), channel_id=1, source_target_pairs={{0,4},{4,8},{8,12},{1,5},{5,9},{9,13},{2,6},{6,10},{10,14},{3,7},{... | collective-permute-start | bytes 245768 | tf_op jit(solution)/shard_map/ppermute | solution.py:16
  53.7 75.7 %all-gather = f32[32,1,4096]{2,1,0:T(1,128)S(1)} all-gather(f32[1,1,4096]{2,1,0:T(1,128)S(1)} %reshape.41), channel_id=1, replica_groups=mesh['cond'=2,'gx'=4,'yz'=4] {'cond','gx','yz'}, dimensions={0}, use_global_device_ids=true | all-gather | bytes 540672 | tf_op jit(solution)/shard_map/all_gather | solution.py:94
  131.5 1.3 collective-permute-start.10
  132.8 4.8 %collective-permute-start.11 = (f32[5,10,1,256]{3,0,2,1:T(8,128)S(1)}, f32[5,10,1,256]{3,0,2,1:T(8,128)S(1)}, u32[]{:S(2)}, u32[]{:S(2)}) collective-permute-start(f32[5,10,1,256]{3,0,2,1:T(8,128)S(1)} %get-tuple-element.11), channel_id=1, source_target_pairs={{0,1},{1,2},{2,3},{4,5},{5,6},{6,7},{8,9},{9,10},{10,11},{12,13},{... | collective-permute-start | bytes 153608 | tf_op jit(solution)/shard_map/ppermute | solution.py:16
  137.6 1.1 convolution_bitcast_fusion
  140.1 1.0 convolution_bitcast_fusion.6
  141.1 1.2 convolution_bitcast_fusion.7
  142.4 1.1 fusion.49
  143.5 1.1 fusion.52
  144.5 2.0 %fusion.86 = f32[1,5,8,16,256]{4,1,3,2,0:T(8,128)S(1)} fusion(f32[5,8,16,256]{3,0,2,1:T(8,128)S(1)} %convolution_bitcast_fusion.6, f32[5,8,16,256]{3,0,2,1:T(8,128)S(1)} %convolution_bitcast_fusion.7, f32[5,8,16,256]{3,0,2,1:T(8,128)S(1)} %fusion.49, f32[5,8,16,256]{3,0,2,1:T(8,128)S(1)} %fusion.52, f32[5,8,16,256]{3,0,2,1:T(8,128)S(1)} %convolution_bitcast_fusion, ...), kind=kOutput, calls=%fused_computation.100 | convolution fusion | flops 11325440 | bytes 5455972 | tf_op jit(solution)/shard_map/ec,exyz->cxyz/dot_general | solution.py:34
  146.5 1.0 copy.69
  (56 shorter events, 9.9 us)
Async XLA Ops:
  0.6 52.5 %copy-start = (f32[256,128]{1,0:T(8,128)S(1)}, f32[256,128]{1,0:T(8,128)}, u32[]{:S(2)}) copy-start(f32[256,128]{1,0:T(8,128)} %param.16) | copy-start | bytes 393220
  0.6 5.9 %copy-start.4 = (f32[1,6,5,5]{1,0,3,2:T(1,128)S(1)}, f32[1,6,5,5]{1,0,3,2:T(1,128)}, u32[]{:S(2)}) copy-start(f32[1,6,5,5]{1,0,3,2:T(1,128)} %param.12) | copy-start | bytes 1804
  0.7 6.9 %copy-start.6 = (s32[8,16]{1,0:T(8,128)S(1)}, s32[8,16]{1,0:T(8,128)}, u32[]{:S(2)}) copy-start(s32[8,16]{1,0:T(8,128)} %param.15) | copy-start | bytes 1540
  2.2 5.4 %collective-permute-start = (f32[5,1,16,256]{3,0,2,1:T(8,128)S(1)}, f32[5,1,16,256]{3,0,2,1:T(8,128)S(1)}, u32[]{:S(2)}, u32[]{:S(2)}) collective-permute-start(f32[5,1,16,256]{3,0,2,1:T(8,128)S(1)} %get-tuple-element.22), channel_id=1, source_target_pairs={{4,0},{8,4},{12,8},{5,1},{9,5},{13,9},{6,2},{10,6},{14,10},{7,3},{... | collective-permute-start | bytes 245768 | tf_op jit(solution)/shard_map/ppermute | solution.py:19
  3.5 4.2 %collective-permute-start.1 = (f32[5,1,16,256]{3,0,2,1:T(8,128)S(1)}, f32[5,1,16,256]{3,0,2,1:T(8,128)S(1)}, u32[]{:S(2)}, u32[]{:S(2)}) collective-permute-start(f32[5,1,16,256]{3,0,2,1:T(8,128)S(1)} %get-tuple-element.21), channel_id=1, source_target_pairs={{0,4},{4,8},{8,12},{1,5},{5,9},{9,13},{2,6},{6,10},{10,14},{3,7},{... | collective-permute-start | bytes 245768 | tf_op jit(solution)/shard_map/ppermute | solution.py:16
  7.7 8.0 %collective-permute-start.2 = (f32[5,10,1,256]{3,0,2,1:T(8,128)S(1)}, f32[5,10,1,256]{3,0,2,1:T(8,128)S(1)}, u32[]{:S(2)}, u32[]{:S(2)}) collective-permute-start(f32[5,10,1,256]{3,0,2,1:T(8,128)S(1)} %get-tuple-element.16), channel_id=1, source_target_pairs={{1,0},{2,1},{3,2},{5,4},{6,5},{7,6},{9,8},{10,9},{11,10},{13,12},{... | collective-permute-start | bytes 153608 | tf_op jit(solution)/shard_map/ppermute | solution.py:19
  9.0 7.6 %collective-permute-start.3 = (f32[5,10,1,256]{3,0,2,1:T(8,128)S(1)}, f32[5,10,1,256]{3,0,2,1:T(8,128)S(1)}, u32[]{:S(2)}, u32[]{:S(2)}) collective-permute-start(f32[5,10,1,256]{3,0,2,1:T(8,128)S(1)} %get-tuple-element.15), channel_id=1, source_target_pairs={{0,1},{1,2},{2,3},{4,5},{5,6},{6,7},{8,9},{9,10},{10,11},{12,13},{... | collective-permute-start | bytes 153608 | tf_op jit(solution)/shard_map/ppermute | solution.py:16
  19.6 2.2 %copy-start.1 = (f32[1,5,8,16,256]{4,3,2,1,0:T(8,128)S(1)}, f32[1,5,8,16,256]{4,3,2,1,0:T(8,128)}, u32[]{:S(2)}) copy-start(f32[1,5,8,16,256]{4,3,2,1,0:T(8,128)} %param.10) | copy-start | bytes 1966084
  19.6 2.2 %copy-start.2 = (f32[8,16,256]{2,1,0:T(8,128)S(1)}, f32[8,16,256]{2,1,0:T(8,128)}, u32[]{:S(2)}) copy-start(f32[8,16,256]{2,1,0:T(8,128)} %param.11) | copy-start | bytes 393220
  21.8 7.2 %copy-start.7 = (s32[2]{0:T(128)S(1)}, s32[2]{0:T(128)}, u32[]{:S(2)}) copy-start(s32[2]{0:T(128)} %param.17) | copy-start | bytes 28
  23.8 7.1 %collective-permute-start.4 = (f32[5,1,16,256]{3,0,2,1:T(8,128)S(1)}, f32[5,1,16,256]{3,0,2,1:T(8,128)S(1)}, u32[]{:S(2)}, u32[]{:S(2)}) collective-permute-start(f32[5,1,16,256]{3,0,2,1:T(8,128)S(1)} %get-tuple-element.20), channel_id=1, source_target_pairs={{4,0},{8,4},{12,8},{5,1},{9,5},{13,9},{6,2},{10,6},{14,10},{7,3},{... | collective-permute-start | bytes 245768 | tf_op jit(solution)/shard_map/ppermute | solution.py:19
  25.1 5.8 %collective-permute-start.5 = (f32[5,1,16,256]{3,0,2,1:T(8,128)S(1)}, f32[5,1,16,256]{3,0,2,1:T(8,128)S(1)}, u32[]{:S(2)}, u32[]{:S(2)}) collective-permute-start(f32[5,1,16,256]{3,0,2,1:T(8,128)S(1)} %get-tuple-element.19), channel_id=1, source_target_pairs={{0,4},{4,8},{8,12},{1,5},{5,9},{9,13},{2,6},{6,10},{10,14},{3,7},{... | collective-permute-start | bytes 245768 | tf_op jit(solution)/shard_map/ppermute | solution.py:16
  30.9 7.2 %collective-permute-start.6 = (f32[5,10,1,256]{3,0,2,1:T(8,128)S(1)}, f32[5,10,1,256]{3,0,2,1:T(8,128)S(1)}, u32[]{:S(2)}, u32[]{:S(2)}) collective-permute-start(f32[5,10,1,256]{3,0,2,1:T(8,128)S(1)} %get-tuple-element.14), channel_id=1, source_target_pairs={{1,0},{2,1},{3,2},{5,4},{6,5},{7,6},{9,8},{10,9},{11,10},{13,12},{... | collective-permute-start | bytes 153608 | tf_op jit(solution)/shard_map/ppermute | solution.py:19
  32.2 6.7 %collective-permute-start.7 = (f32[5,10,1,256]{3,0,2,1:T(8,128)S(1)}, f32[5,10,1,256]{3,0,2,1:T(8,128)S(1)}, u32[]{:S(2)}, u32[]{:S(2)}) collective-permute-start(f32[5,10,1,256]{3,0,2,1:T(8,128)S(1)} %get-tuple-element.13), channel_id=1, source_target_pairs={{0,1},{1,2},{2,3},{4,5},{5,6},{6,7},{8,9},{9,10},{10,11},{12,13},{... | collective-permute-start | bytes 153608 | tf_op jit(solution)/shard_map/ppermute | solution.py:16
  41.8 2.2 %copy-start.3 = (bf16[1,5,8,16,256]{4,3,2,1,0:T(8,128)(2,1)S(1)}, bf16[1,5,8,16,256]{4,3,2,1,0:T(8,128)(2,1)}, u32[]{:S(2)}) copy-start(bf16[1,5,8,16,256]{4,3,2,1,0:T(8,128)(2,1)} %param.13) | copy-start | bytes 983044
  44.0 9.1 %copy-start.5 = (s32[8,16,256]{2,1,0:T(8,128)S(1)}, s32[8,16,256]{2,1,0:T(8,128)}, u32[]{:S(2)}) copy-start(s32[8,16,256]{2,1,0:T(8,128)} %param.14) | copy-start | bytes 393220
  46.2 85.3 %collective-permute-start.8 = (f32[5,1,16,256]{3,0,2,1:T(8,128)S(1)}, f32[5,1,16,256]{3,0,2,1:T(8,128)S(1)}, u32[]{:S(2)}, u32[]{:S(2)}) collective-permute-start(f32[5,1,16,256]{3,0,2,1:T(8,128)S(1)} %get-tuple-element.18), channel_id=1, source_target_pairs={{4,0},{8,4},{12,8},{5,1},{9,5},{13,9},{6,2},{10,6},{14,10},{7,3},{... | collective-permute-start | bytes 245768 | tf_op jit(solution)/shard_map/ppermute | solution.py:19
  47.5 84.0 %collective-permute-start.9 = (f32[5,1,16,256]{3,0,2,1:T(8,128)S(1)}, f32[5,1,16,256]{3,0,2,1:T(8,128)S(1)}, u32[]{:S(2)}, u32[]{:S(2)}) collective-permute-start(f32[5,1,16,256]{3,0,2,1:T(8,128)S(1)} %get-tuple-element.17), channel_id=1, source_target_pairs={{0,4},{4,8},{8,12},{1,5},{5,9},{9,13},{2,6},{6,10},{10,14},{3,7},{... | collective-permute-start | bytes 245768 | tf_op jit(solution)/shard_map/ppermute | solution.py:16
  131.5 7.2 %collective-permute-start.10 = (f32[5,10,1,256]{3,0,2,1:T(8,128)S(1)}, f32[5,10,1,256]{3,0,2,1:T(8,128)S(1)}, u32[]{:S(2)}, u32[]{:S(2)}) collective-permute-start(f32[5,10,1,256]{3,0,2,1:T(8,128)S(1)} %get-tuple-element.12), channel_id=1, source_target_pairs={{1,0},{2,1},{3,2},{5,4},{6,5},{7,6},{9,8},{10,9},{11,10},{13,12},{... | collective-permute-start | bytes 153608 | tf_op jit(solution)/shard_map/ppermute | solution.py:19
  132.8 6.6 %collective-permute-start.11 = (f32[5,10,1,256]{3,0,2,1:T(8,128)S(1)}, f32[5,10,1,256]{3,0,2,1:T(8,128)S(1)}, u32[]{:S(2)}, u32[]{:S(2)}) collective-permute-start(f32[5,10,1,256]{3,0,2,1:T(8,128)S(1)} %get-tuple-element.11), channel_id=1, source_target_pairs={{0,1},{1,2},{2,3},{4,5},{5,6},{6,7},{8,9},{9,10},{10,11},{12,13},{... | collective-permute-start | bytes 153608 | tf_op jit(solution)/shard_map/ppermute | solution.py:16
